TPU v7x, 32 devices: a whole 2x2x4 slice. The times are simulated.
32 devices in a mesh: fsdp: 8 (over z, y), tp: 4 (over x, core).
Axes of the slice: x: 2, y: 2, z: 4, core: 2. Of those that a mesh axis runs over, the one named last changes fastest.
Arguments:
- base_o: bfloat16 [2, 8192, 8192], P(None, 'tp', 'fsdp'), may hold values from -0.0625 to 0.0625
- base_down: bfloat16 [2, 28672, 8192], P(None, 'tp', 'fsdp'), may hold values from -0.03125 to 0.03125
- factor_a_o: bfloat16 [2, 64, 4, 2048], P(None, None, None, 'fsdp'), may hold values from -0.0625 to 0.0625
- factor_b_o: bfloat16 [2, 8192, 64], P(None, 'fsdp'), may hold values from -1.1953125 to 1.1953125
- factor_a_down: bfloat16 [2, 64, 4, 7168], P(None, None, None, 'fsdp'), may hold values from -0.03125 to 0.03125
- factor_b_down: bfloat16 [2, 8192, 64], P(None, 'fsdp'), may hold values from -1.1953125 to 1.1953125
- magnitude_o: float32 [2, 8192], P(None, 'fsdp'), may hold values from 30 to 300
- magnitude_down: float32 [2, 8192], P(None, 'fsdp'), may hold values from 30 to 300
Outputs:
- merged_o: bfloat16 [2, 8192, 8192], P(None, 'tp', 'fsdp')
- merged_down: bfloat16 [2, 28672, 8192], P(None, 'tp', 'fsdp')
All inputs are finite; a program needn't handle non-finite values.
Results may differ from a plain program's by a relative error of at most 0.001.
Values may be sent and summed in bfloat16 or wider, within the bound.
A program may use at most 192 MiB of HBM per device.

v0:
```python
import jax
import jax.numpy as jnp
from jax import lax
from jax.sharding import PartitionSpec as P


def low_rank(rows_a, factor_b):
    return jnp.einsum("lri,lor->lio", rows_a, factor_b, preferred_element_type=jnp.float32)


def squares(base, delta):
    summed = base.astype(jnp.float32) + 0.25 * delta
    return (summed, jnp.sum(summed * summed, axis=1))


def finish(summed, square, magnitude):
    return (magnitude[:, None, :] * summed * lax.rsqrt(square + 1e-06)[:, None, :]).astype(
        jnp.bfloat16
    )


def local(
    base_o,
    base_down,
    factor_a_o,
    factor_b_o,
    factor_a_down,
    factor_b_down,
    magnitude_o,
    magnitude_down,
):
    column_t = lax.axis_index("tp")
    own_o = lax.dynamic_index_in_dim(factor_a_o, column_t, 2, keepdims=False)
    delta_o = low_rank(lax.all_gather(own_o, "fsdp", axis=2, tiled=True), factor_b_o)
    own_down = lax.dynamic_index_in_dim(factor_a_down, column_t, 2, keepdims=False)
    delta_down = low_rank(lax.all_gather(own_down, "fsdp", axis=2, tiled=True), factor_b_down)
    summed_o, partial_o = squares(base_o, delta_o)
    square_o = lax.psum(partial_o, "tp")
    merged_o = finish(summed_o, square_o, magnitude_o)
    summed_down, partial_down = squares(base_down, delta_down)
    square_down = lax.psum(partial_down, "tp")
    merged_down = finish(summed_down, square_down, magnitude_down)
    return (merged_o, merged_down)


def solution(mesh):
    return jax.shard_map(
        local,
        mesh=mesh,
        in_specs=(
            P(None, "tp", "fsdp"),
            P(None, "tp", "fsdp"),
            P(None, None, None, "fsdp"),
            P(None, "fsdp", None),
            P(None, None, None, "fsdp"),
            P(None, "fsdp", None),
            P(None, "fsdp"),
            P(None, "fsdp"),
        ),
        out_specs=(P(None, "tp", "fsdp"), P(None, "tp", "fsdp")),
        check_vma=False,
    )
```

profile of v0, /device:TPU:0, one launch (start us, length us, event | category | flops | bytes accessed | tf_op | source)
XLA Modules:
  0.0 159.7 jit_solution(17813612528903440651)
XLA Ops:
  7.2 0.0 copy-start
  7.2 0.0 copy-start.2
  7.2 0.0 all-gather.4.cloned.1.call-start
  7.2 1.1 copy-done
  8.4 0.5 constant_dynamic-slice_fusion
  8.8 0.7 copy.13
  9.5 0.0 all-gather.4.cloned.1.call-update
  9.6 1.1 constant_dynamic-slice_fusion.1
  10.7 33.7 %all-gather = bf16[2,64,1,2048]{3,1,0,2:T(8,128)(2,1)S(1)} all-gather(bf16[2,64,1,256]{3,1,0,2:T(8,128)(2,1)S(1)} %copy.12), channel_id=2, replica_groups=mesh['fsdp'=8,'tp'=4] {'fsdp'}, dimensions={3}, use_global_device_ids=true | all-gather | bytes 589824 | tf_op jit(solution)/shard_map/all_gather | solution.py:34
  44.4 10.1 %multiply_reduce_fusion.1 = (f32[2,1024]{1,0:T(2,128)S(1)}, f32[2,2048,1024]{2,1,0:T(8,128)}) fusion(bf16[2,2048,1024]{2,1,0:T(8,128)(2,1)} %param.8, bf16[2,1024,64]{1,2,0:T(8,128)(2,1)} %param.11, bf16[2,64,1,2048]{3,1,0,2:T(8,128)(2,1)S(1)} %all-gather), kind=kOutput, calls=%fused_computation.4 | convolution fusion | flops 557840384 | bytes 25960448 | tf_op jit(solution)/shard_map/lri,lor->lio/dot_general | solution.py:8
  54.5 0.0 copy-start.4
  54.5 7.0 %all-gather.4.cloned.1.call-done = bf16[2,64,1,7168]{3,1,0,2:T(8,128)(2,1)} async-done(((bf16[2,64,1,896]{3,1,0,2:T(8,128)(2,1)}), bf16[2,64,1,7168]{3,1,0,2:T(8,128)(2,1)}) %all-gather.4.cloned.1.call-update) | async-done | bytes 1835024 | tf_op jit(solution)/shard_map/all_gather | solution.py:36
  61.5 0.0 copy-done.2
  61.5 30.8 %multiply_reduce_fusion = (f32[2,1024]{1,0:T(2,128)S(1)}, f32[2,7168,1024]{2,1,0:T(8,128)}) fusion(bf16[2,7168,1024]{2,1,0:T(8,128)(2,1)} %param.9, bf16[2,1024,64]{1,2,0:T(8,128)(2,1)S(1)} %copy-done.2, bf16[2,64,1,7168]{3,1,0,2:T(8,128)(2,1)} %all-gather.4.cloned.1.call-done), kind=kOutput, calls=%fused_computation.1 | convolution fusion | flops 1952446464 | bytes 90185728 | tf_op jit(solution)/shard_map/lri,lor->lio/dot_general | solution.py:8
  92.3 10.1 %all-reduce = (f32[2,1024]{1,0:T(2,128)S(1)}, f32[2,1024]{1,0:T(2,128)S(1)}) all-reduce(f32[2,1024]{1,0:T(2,128)S(1)} %get-tuple-element.4, f32[2,1024]{1,0:T(2,128)S(1)} %get-tuple-element.6), channel_id=1, replica_groups=mesh['fsdp'=8,'tp'=4] {'tp'}, use_global_device_ids=true, to_apply=%region_1.2 | all-reduce | flops 4096 | bytes 32768 | tf_op jit(solution)/shard_map/psum | solution.py:38
  102.5 0.0 copy-done.4
  102.5 0.0 copy-start.3
  102.5 12.2 %multiply_convert_fusion.1 = bf16[2,2048,1024]{2,1,0:T(8,128)(2,1)} fusion(f32[2,2048,1024]{2,1,0:T(8,128)} %get-tuple-element.5, bf16[2,2048,1024]{2,1,0:T(8,128)(2,1)} %param.8, f32[2,1024]{1,0:T(2,128)S(1)} %get-tuple-element.9, f32[2,1024]{1,0:T(2,128)S(1)} %copy-done.4), kind=kLoop, calls=%fused_computation.3 | loop fusion | flops 25165824 | bytes 33570816 | tf_op jit(solution)/shard_map/convert_element_type | solution.py:17
  114.7 0.0 copy-done.3
  114.7 0.0 copy-start.1
  114.7 38.2 %multiply_convert_fusion = bf16[2,7168,1024]{2,1,0:T(8,128)(2,1)} fusion(f32[2,7168,1024]{2,1,0:T(8,128)} %get-tuple-element.7, bf16[2,7168,1024]{2,1,0:T(8,128)(2,1)} %param.9, f32[2,1024]{1,0:T(2,128)S(1)} %get-tuple-element.8, f32[2,1024]{1,0:T(2,128)S(1)} %copy-done.3), kind=kLoop, calls=%fused_computation | loop fusion | flops 88080384 | bytes 117456896 | tf_op jit(solution)/shard_map/convert_element_type | solution.py:17
  152.8 0.0 copy-done.1
  (2 shorter events, 0.0 us)
Async XLA Ops:
  7.2 1.2 copy-start
  7.2 54.3 %copy-start.2 = (bf16[2,1024,64]{1,2,0:T(8,128)(2,1)S(1)}, bf16[2,1024,64]{1,2,0:T(8,128)(2,1)}, u32[]{:S(2)}) copy-start(bf16[2,1024,64]{1,2,0:T(8,128)(2,1)} %param.13) | copy-start | bytes 786436
  7.2 54.3 %all-gather.4.cloned.1.call-start = ((), (), s32[]{:S(2)}) async-start(), calls=%async_computation | async-start | bytes 2064384 | tf_op jit(solution)/shard_map/all_gather | solution.py:36
  54.5 48.0 %copy-start.4 = (f32[2,1024]{1,0:T(2,128)S(1)}, f32[2,1024]{1,0:T(2,128)}, u32[]{:S(2)}) copy-start(f32[2,1024]{1,0:T(2,128)} %param.14) | copy-start | bytes 24580
  102.5 12.2 %copy-start.3 = (f32[2,1024]{1,0:T(2,128)S(1)}, f32[2,1024]{1,0:T(2,128)}, u32[]{:S(2)}) copy-start(f32[2,1024]{1,0:T(2,128)} %param.15) | copy-start | bytes 24580
  114.7 38.2 %copy-start.1 = (bf16[2,64,4,896]{3,2,1,0:T(4,128)(2,1)S(1)}, bf16[2,64,4,896]{3,2,1,0:T(4,128)(2,1)}, u32[]{:S(2)}) copy-start(bf16[2,64,4,896]{3,2,1,0:T(4,128)(2,1)} %param.12) | copy-start | bytes 2752516
Sparse Core Ops, SparseCore 0:
  10.8 50.6 all-gather.3
where the time goes:
time: 160 us
  other arithmetic  50.4 us (32%)
  blocking collectives  43.8 us (27%)
  matrix products  40.9 us (26%)
  between operations  14.1 us (9%)
  waiting for transfers between devices  7.03 us (4%)
  local copies, waits for them, and re-layouts  3.44 us (2%)
    convert_element_type x2, other arithmetic, finish(): (magnitude[:, None, :] * summed * lax.rsqrt(square + 1e-06)[:, None, :])....  50.4 us
    dot_general x2, matrix products, low_rank(): jnp.einsum('lri,lor->lio', rows_a, factor_b, preferred_element_type=jnp.f...  40.9 us
    all_gather x1, blocking collectives, local(): lax.all_gather(own_o, 'fsdp', axis=2, tiled=True)  33.7 us
    psum x1, blocking collectives, local(): square_o = lax.psum(partial_o, 'tp')  10.1 us
    all_gather x1, waiting for transfers between devices, local(): lax.all_gather(own_down, 'fsdp', axis=2, tiled=True)  7.01 us
  transfers between devices with their start and end apart: 1, of which 1 were waited for; matrix products, arithmetic and copies ran while one was open for 7% of the time, Pallas kernels for 0%

commit v1 on v0

--- a/solution.py
+++ b/solution.py
@@ -35,7 +35,9 @@
     own_down = lax.dynamic_index_in_dim(factor_a_down, column_t, 2, keepdims=False)
     delta_down = low_rank(lax.all_gather(own_down, "fsdp", axis=2, tiled=True), factor_b_down)
     summed_o, partial_o = squares(base_o, delta_o)
-    square_o = lax.psum(partial_o, "tp")
+    square_o = partial_o
+    for hop in (1, 2):
+        square_o = square_o + lax.ppermute(square_o, "tp", [(dev, dev ^ hop) for dev in range(4)])
     merged_o = finish(summed_o, square_o, magnitude_o)
     summed_down, partial_down = squares(base_down, delta_down)
     square_down = lax.psum(partial_down, "tp")

time: 160 us -> 144 us (0.900)
  other arithmetic: 50.4 us -> 44.2 us
  matrix products: 40.9 us -> 36.8 us
  blocking collectives: 43.8 us -> 39.8 us
  waiting for transfers between devices: 7.03 us -> 3.34 us
    all_gather x1, waiting for transfers between devices: 7.01 us -> 0.01 us  [local(): lax.all_gather(own_down, 'fsdp', axis=2, tiled=True)]
    convert_element_type x2, other arithmetic: 50.4 us -> 44.1 us  [finish(): (magnitude[:, None, :] * summed * lax.rsqrt(square + 1e-06)[:, None, :])....]
    psum x1, blocking collectives: 10.1 us -> 5.87 us  [local(): square_down = lax.psum(partial_down, 'tp')]
    dot_general x2, matrix products: 40.9 us -> 36.8 us  [low_rank(): jnp.einsum('lri,lor->lio', rows_a, factor_b, preferred_element_type=jnp.f...]
    ppermute x0 -> x2, waiting for transfers between devices: none -> 3.32 us  [local(): lax.ppermute(square_o, 'tp', [(dev, dev ^ hop) for dev in range(4)])]
  transfers between devices with their start and end apart: 1 -> 3, of which waited for: 1 -> 2; matrix products, arithmetic and copies ran while one was open for 7% -> 9% of each run, Pallas kernels for 0% -> 0%
where the time goes in v1:
time: 144 us; the launch traced here: 143 us
  other arithmetic  44.2 us (31%)
  blocking collectives  39.8 us (28%)
  matrix products  36.8 us (26%)
  between operations  14.2 us (10%)
  local copies, waits for them, and re-layouts  3.6 us (2%)
  waiting for transfers between devices  3.34 us (2%)
  starting transfers between devices  1.6 us (1%)
    convert_element_type x2, other arithmetic, finish(): (magnitude[:, None, :] * summed * lax.rsqrt(square + 1e-06)[:, None, :])....  44.1 us
    dot_general x2, matrix products, low_rank(): jnp.einsum('lri,lor->lio', rows_a, factor_b, preferred_element_type=jnp.f...  36.8 us
    all_gather x1, blocking collectives, local(): lax.all_gather(own_o, 'fsdp', axis=2, tiled=True)  33.9 us
    psum x1, blocking collectives, local(): square_down = lax.psum(partial_down, 'tp')  5.87 us
    ppermute x2, waiting for transfers between devices, local(): lax.ppermute(square_o, 'tp', [(dev, dev ^ hop) for dev in range(4)])  3.32 us
  transfers between devices with their start and end apart: 3, of which 2 were waited for; matrix products, arithmetic and copies ran while one was open for 9% of the time, Pallas kernels for 0%

profile of v1, /device:TPU:0, one launch (start us, length us, event | category | flops | bytes accessed | tf_op | source)
XLA Modules:
  0.0 143.4 jit_solution(4051045481012012978)
XLA Ops:
  7.2 0.0 copy-start
  7.2 0.0 copy-start.4
  7.2 0.0 all-gather.4.cloned.1.call-start
  7.2 1.1 copy-done
  8.4 0.5 constant_dynamic-slice_fusion
  8.8 0.7 copy.13
  9.5 0.0 all-gather.4.cloned.1.call-update
  9.6 0.0 slice-start
  9.6 1.2 constant_dynamic-slice_fusion.1
  10.9 33.9 %all-gather = bf16[2,64,1,2048]{3,1,0,2:T(8,128)(2,1)S(1)} all-gather(bf16[2,64,1,256]{3,1,0,2:T(8,128)(2,1)S(1)} %copy.12), channel_id=2, replica_groups=mesh['fsdp'=8,'tp'=4] {'fsdp'}, dimensions={3}, use_global_device_ids=true | all-gather | bytes 589824 | tf_op jit(solution)/shard_map/all_gather | solution.py:34
  44.8 0.0 slice-start.1
  44.8 5.9 %multiply_reduce_fusion.1 = (f32[2,1024]{1,0:T(2,128)S(1)}, f32[2,2048,1024]{2,1,0:T(8,128)S(1)}) fusion(bf16[2,2048,1024]{2,1,0:T(8,128)(2,1)} %param.8, bf16[2,1024,64]{1,2,0:T(8,128)(2,1)} %param.11, bf16[2,64,1,2048]{3,1,0,2:T(8,128)(2,1)S(1)} %all-gather), kind=kOutput, calls=%fused_computation.4 | convolution fusion | flops 557840384 | bytes 25960448 | tf_op jit(solution)/shard_map/lri,lor->lio/dot_general | solution.py:8
  50.7 0.1 collective-permute-start
  50.8 1.2 collective-permute-done
  52.0 1.5 %collective-permute-start.1 = (f32[2,1024]{1,0:T(2,128)S(1)}, f32[2,1024]{1,0:T(2,128)S(1)}, u32[]{:S(2)}, u32[]{:S(2)}) collective-permute-start(f32[2,1024]{1,0:T(2,128)S(1)} %add.28), channel_id=1, source_target_pairs={{0,2},{1,3},{2,0},{3,1},{4,6},{5,7},{6,4},{7,5},{8,10},{9,11},{10,... | collective-permute-start | bytes 24584 | tf_op jit(solution)/shard_map/ppermute | solution.py:40
  53.4 2.2 %collective-permute-done.1 = f32[2,1024]{1,0:T(2,128)S(1)} collective-permute-done((f32[2,1024]{1,0:T(2,128)S(1)}, f32[2,1024]{1,0:T(2,128)S(1)}, u32[]{:S(2)}, u32[]{:S(2)}) %collective-permute-start.1) | collective-permute-done | bytes 8224 | tf_op jit(solution)/shard_map/ppermute | solution.py:40
  55.6 0.0 copy-done.4
  55.6 0.0 slice-done
  55.6 0.0 slice-done.1
  55.7 0.0 copy-start.2
  55.7 6.0 %multiply_convert_fusion.1 = bf16[2,2048,1024]{2,1,0:T(8,128)(2,1)} fusion(f32[2,2048,1024]{2,1,0:T(8,128)S(1)} %get-tuple-element.3, bf16[2,2048,1024]{2,1,0:T(8,128)(2,1)S(1)} %bitcast.13, f32[2,1024]{1,0:T(2,128)S(1)} %add_rsqrt_fusion.1, f32[2,1024]{1,0:T(2,128)S(1)} %copy-done.4), kind=kLoop, calls=%fused_computation.3 | loop fusion | flops 25165824 | bytes 33570816 | tf_op jit(solution)/shard_map/convert_element_type | solution.py:17
  61.6 0.0 copy-start.3
  61.6 0.0 all-gather.4.cloned.1.call-done
  61.6 0.0 copy-done.2
  61.6 30.8 %multiply_reduce_fusion = (f32[2,1024]{1,0:T(2,128)S(1)}, f32[2,7168,1024]{2,1,0:T(8,128)}) fusion(bf16[2,7168,1024]{2,1,0:T(8,128)(2,1)} %param.9, bf16[2,1024,64]{1,2,0:T(8,128)(2,1)S(1)} %copy-done.2, bf16[2,64,1,7168]{3,1,0,2:T(8,128)(2,1)} %all-gather.4.cloned.1.call-done), kind=kOutput, calls=%fused_computation.1 | convolution fusion | flops 1952446464 | bytes 90185728 | tf_op jit(solution)/shard_map/lri,lor->lio/dot_general | solution.py:8
  92.5 5.9 %psum.7 = f32[2,1024]{1,0:T(2,128)S(1)} all-reduce(f32[2,1024]{1,0:T(2,128)S(1)} %get-tuple-element.4), channel_id=1, replica_groups=mesh['fsdp'=8,'tp'=4] {'tp'}, use_global_device_ids=true, to_apply=%region_2.3 | all-reduce | flops 2048 | bytes 16384 | tf_op jit(solution)/shard_map/psum | solution.py:43
  98.3 0.0 copy-done.3
  98.4 0.0 copy-start.1
  98.4 38.2 %multiply_convert_fusion = bf16[2,7168,1024]{2,1,0:T(8,128)(2,1)} fusion(f32[2,7168,1024]{2,1,0:T(8,128)} %get-tuple-element.5, bf16[2,7168,1024]{2,1,0:T(8,128)(2,1)} %param.9, f32[2,1024]{1,0:T(2,128)S(1)} %add_rsqrt_fusion, f32[2,1024]{1,0:T(2,128)S(1)} %copy-done.3), kind=kLoop, calls=%fused_computation | loop fusion | flops 88080384 | bytes 117456896 | tf_op jit(solution)/shard_map/convert_element_type | solution.py:17
  136.6 0.0 copy-done.1
  (5 shorter events, 0.0 us)
Async XLA Ops:
  7.2 1.2 copy-start
  7.2 48.4 %copy-start.4 = (f32[2,1024]{1,0:T(2,128)S(1)}, f32[2,1024]{1,0:T(2,128)}, u32[]{:S(2)}) copy-start(f32[2,1024]{1,0:T(2,128)} %param.14) | copy-start | bytes 24580
  7.2 54.4 %all-gather.4.cloned.1.call-start = ((), (), s32[]{:S(2)}) async-start(), calls=%async_computation | async-start | bytes 2064384 | tf_op jit(solution)/shard_map/all_gather | solution.py:36
  9.6 46.1 %slice-start = ((s8[8388608]{0:T(1024)(128)(4,1)}), s8[4194304]{0:T(1024)(128)(4,1)S(1)}, s32[]{:S(2)}) async-start(s8[8388608]{0:T(1024)(128)(4,1)} %bitcast.12), calls=%async_computation.1 | async-start | bytes 8388608
  44.8 10.9 %slice-start.1 = ((s8[8388608]{0:T(1024)(128)(4,1)}), s8[4194304]{0:T(1024)(128)(4,1)S(1)}, s32[]{:S(2)}) async-start(s8[8388608]{0:T(1024)(128)(4,1)} %bitcast.12), calls=%async_computation.2 | async-start | bytes 8388608
  50.7 1.2 collective-permute-start
  52.0 3.7 %collective-permute-start.1 = (f32[2,1024]{1,0:T(2,128)S(1)}, f32[2,1024]{1,0:T(2,128)S(1)}, u32[]{:S(2)}, u32[]{:S(2)}) collective-permute-start(f32[2,1024]{1,0:T(2,128)S(1)} %add.28), channel_id=1, source_target_pairs={{0,2},{1,3},{2,0},{3,1},{4,6},{5,7},{6,4},{7,5},{8,10},{9,11},{10,... | collective-permute-start | bytes 24584 | tf_op jit(solution)/shard_map/ppermute | solution.py:40
  55.7 6.0 %copy-start.2 = (bf16[2,1024,64]{1,2,0:T(8,128)(2,1)S(1)}, bf16[2,1024,64]{1,2,0:T(8,128)(2,1)}, u32[]{:S(2)}) copy-start(bf16[2,1024,64]{1,2,0:T(8,128)(2,1)} %param.13) | copy-start | bytes 786436
  61.6 36.7 %copy-start.3 = (f32[2,1024]{1,0:T(2,128)S(1)}, f32[2,1024]{1,0:T(2,128)}, u32[]{:S(2)}) copy-start(f32[2,1024]{1,0:T(2,128)} %param.15) | copy-start | bytes 24580
  98.4 38.2 %copy-start.1 = (bf16[2,64,4,896]{3,2,1,0:T(4,128)(2,1)S(1)}, bf16[2,64,4,896]{3,2,1,0:T(4,128)(2,1)}, u32[]{:S(2)}) copy-start(bf16[2,64,4,896]{3,2,1,0:T(4,128)(2,1)} %param.12) | copy-start | bytes 2752516
Sparse Core Ops, SparseCore 0:
  10.8 50.3 all-gather.3
